TPU v7x, 32 devices: a whole 2x2x4 slice. The times are simulated.
32 devices in a mesh: row: 4 (over y, core), col: 8 (over z, x).
Axes of the slice: x: 2, y: 2, z: 4, core: 2. Of those that a mesh axis runs over, the one named last changes fastest.
Arguments:
- blocks: float32 [4096, 128, 128], P(('row', 'col')), may hold values from -0.25 to 0.25
- block_rows: int32 [32, 128], P(('row', 'col')), may hold values from 0 to 1023, as said below
- block_cols: int32 [32, 128], P(('row', 'col')), may hold values from 0 to 511
- diagonal: float32 [524288], P(('row', 'col')), may hold values from 1 to 4
- right_sides: float32 [2, 524288], P(None, ('row', 'col')), may hold values from -6 to 6
Outputs:
- solution: float32 [2, 524288], P(None, ('row', 'col'))
- hessenberg: float32 [2, 9, 8], replicated
Inputs may be any that keep to these rules, and one draw needn't show every extreme that they name: `block_rows`: non-decreasing along each tile's slots; a local block row may hold no stored block.
All inputs are finite; a program needn't handle non-finite values.
Results may differ from a plain program's by a relative error of at most 0.0085.
Values sent between devices are 32-bit elements; how exact they have to be, the bound alone decides.
A program may use at most 128 MiB of HBM per device.

v0:
```python
import jax
import jax.numpy as jnp
from jax import lax
from jax.sharding import PartitionSpec as P

STEPS = 8
epsilon = 1e-06


def least_squares(hessenberg, initial_norm):
    total_steps = hessenberg.shape[2]
    targets = [initial_norm] + [jnp.zeros_like(initial_norm) for j in range(total_steps)]
    cosines, sines, triangle = ([], [], [])
    for j in range(total_steps):
        column = [hessenberg[:, i, j] for i in range(j + 2)]
        for i in range(j):
            leading, trailing = (column[i], column[i + 1])
            column[i] = cosines[i] * leading + sines[i] * trailing
            column[i + 1] = cosines[i] * trailing - sines[i] * leading
        radius = jnp.sqrt(column[j] * column[j] + column[j + 1] * column[j + 1])
        cosine = column[j] / radius
        sine_term = column[j + 1] / radius
        column[j] = radius
        cosines.append(cosine)
        sines.append(sine_term)
        targets[j + 1] = -sine_term * targets[j]
        targets[j] = cosine * targets[j]
        triangle.append(column[: j + 1])
    coeffs = [None] * total_steps
    for j in reversed(range(total_steps)):
        running = targets[j]
        for k in range(j + 1, total_steps):
            running = running - triangle[k][j] * coeffs[k]
        coeffs[j] = running / triangle[j][j]
    return jnp.stack(coeffs, axis=1)


def apply_matrix(vector, blocks, rows_onehot, block_cols, diagonal):
    systems = vector.shape[0]
    width = blocks.shape[1]
    gathered = lax.all_gather(vector, "row", axis=1, tiled=True)
    grouped = gathered.reshape(systems, -1, width)
    picked = jnp.take(grouped, block_cols, axis=1)
    products = jnp.einsum("kij,nkj->nki", blocks, picked, precision=lax.Precision.HIGHEST)
    own_rows = lax.psum_scatter(
        jnp.einsum("mk,nki->mni", rows_onehot, products, precision=lax.Precision.HIGHEST),
        "col",
        scatter_dimension=0,
        tiled=True,
    )
    summed = jnp.transpose(own_rows, (1, 0, 2)).reshape(systems, -1)
    return diagonal[None, :] * vector + summed


def body(blocks, block_rows, block_cols, diagonal, right_sides):
    systems = right_sides.shape[0]
    width = blocks.shape[1]
    row_count = lax.axis_size("col") * (right_sides.shape[1] // width)
    positions = jnp.arange(row_count, dtype=jnp.int32)
    rows_onehot = (block_rows[0][None, :] == positions[:, None]).astype(jnp.float32)
    columns_local = block_cols[0]
    total_steps = STEPS
    initial_norm = jnp.sqrt(
        lax.psum(jnp.sum(right_sides * right_sides, axis=1), ("row", "col")) + epsilon
    )
    krylov_basis = [right_sides / initial_norm[:, None]]
    hessenberg = jnp.zeros((systems, total_steps + 1, total_steps), jnp.float32)
    for j in range(total_steps):
        candidate = apply_matrix(krylov_basis[j], blocks, rows_onehot, columns_local, diagonal)
        stacked = jnp.stack(krylov_basis)
        local_dots = jnp.einsum("inl,nl->ni", stacked, candidate, precision=lax.Precision.HIGHEST)
        coeffs = lax.psum(local_dots, ("row", "col"))
        candidate = candidate - jnp.einsum(
            "ni,inl->nl", coeffs, stacked, precision=lax.Precision.HIGHEST
        )
        remainder_sq = lax.psum(jnp.sum(candidate * candidate, axis=1), ("row", "col"))
        new_norm = jnp.sqrt(remainder_sq + epsilon)
        hessenberg = hessenberg.at[:, : j + 1, j].set(coeffs)
        hessenberg = hessenberg.at[:, j + 1, j].set(new_norm)
        krylov_basis.append(candidate / new_norm[:, None])
    weights = least_squares(hessenberg, initial_norm)
    solution = jnp.einsum(
        "ni,inl->nl",
        weights,
        jnp.stack(krylov_basis[:total_steps]),
        precision=lax.Precision.HIGHEST,
    )
    return (solution, hessenberg)


def solution(mesh):
    return jax.shard_map(
        body,
        mesh=mesh,
        in_specs=(
            P(("row", "col"), None, None),
            P(("row", "col"), None),
            P(("row", "col"), None),
            P(("row", "col")),
            P(None, ("row", "col")),
        ),
        out_specs=(P(None, ("row", "col")), P()),
        check_vma=False,
    )
```

profile of v0, /device:TPU:0, one launch (start us, length us, event | category | flops | bytes accessed | tf_op | source)
XLA Modules:
  0.0 1472.0 jit_solution(12052770710032486379)
XLA Ops:
  9.7 41.9 %psum.119 = f32[2]{0:T(128)S(1)} all-reduce(f32[2]{0:T(128)S(1)} %multiply_reduce_fusion.8), channel_id=1, replica_groups=mesh['row'=4,'col'=8] {'row','col'}, use_global_device_ids=true, to_apply=%region_1.0 | all-reduce | flops 2 | bytes 16 | tf_op jit(solution)/shard_map/psum | solution.py:64
  52.7 7.9 all_gather.24
  61.4 15.5 %convolution_bitcast_fusion.7 = f32[2,128,128]{2,0,1:T(2,128)S(1)} fusion(f32[128,128,128]{2,1,0:T(8,128)} %param.39, f32[128,2,128]{2,1,0:T(2,128)S(1)} %gather_fusion, pred[128]{0:T(512)(128)(4,1)S(1)} %compare_and_fusion), kind=kOutput, calls=%fused_computation.19 | convolution fusion | flops 50364416 | bytes 8650880 | tf_op jit(solution)/shard_map/kij,nkj->nki/dot_general | solution.py:44
  79.3 62.7 %reduce-scatter.9.cloned.1.call-done = f32[128,2,128]{2,0,1:T(8,128)} async-done(((f32[1024,2,128]{2,0,1:T(8,128)}), f32[128,2,128]{2,0,1:T(8,128)}) %reduce-scatter.9.cloned.1.call-update) | async-done | bytes 131088 | tf_op jit(solution)/shard_map/reduce_scatter | solution.py:45
  143.1 39.9 %psum.120 = f32[2,1]{0,1:T(1,128)S(1)} all-reduce(f32[2,1]{0,1:T(1,128)S(1)} %bitcast.742), channel_id=1, replica_groups=mesh['row'=4,'col'=8] {'row','col'}, use_global_device_ids=true, to_apply=%region_3.5 | all-reduce | flops 2 | bytes 16 | tf_op jit(solution)/shard_map/psum | solution.py:72
  184.2 39.2 %psum.121 = f32[2]{0:T(128)S(1)} all-reduce(f32[2]{0:T(128)S(1)} %get-tuple-element.266), channel_id=1, replica_groups=mesh['row'=4,'col'=8] {'row','col'}, use_global_device_ids=true, to_apply=%region_5.7 | all-reduce | flops 2 | bytes 16 | tf_op jit(solution)/shard_map/psum | solution.py:76
  223.6 8.1 all_gather.25
  232.5 15.5 %convolution_bitcast_fusion.6 = f32[2,128,128]{2,0,1:T(2,128)S(1)} fusion(f32[128,128,128]{2,1,0:T(8,128)} %param.39, f32[128,2,128]{2,1,0:T(2,128)S(1)} %gather_fusion.1, pred[128]{0:T(512)(128)(4,1)S(1)} %compare_and_fusion), kind=kOutput, calls=%fused_computation.18 | convolution fusion | flops 50364416 | bytes 8650880 | tf_op jit(solution)/shard_map/kij,nkj->nki/dot_general | solution.py:44
  251.0 61.7 %reduce-scatter.11.cloned.1.call-done = f32[128,2,128]{2,0,1:T(8,128)} async-done(((f32[1024,2,128]{2,0,1:T(8,128)}), f32[128,2,128]{2,0,1:T(8,128)}) %reduce-scatter.11.cloned.1.call-update) | async-done | bytes 131088 | tf_op jit(solution)/shard_map/reduce_scatter | solution.py:45
  313.8 2.5 fusion.53
  316.2 39.8 %psum.122 = f32[2,2]{1,0:T(2,128)S(1)} all-reduce(f32[2,2]{1,0:T(2,128)S(1)} %bitcast.732), channel_id=1, replica_groups=mesh['row'=4,'col'=8] {'row','col'}, use_global_device_ids=true, to_apply=%region_7.9 | all-reduce | flops 4 | bytes 32 | tf_op jit(solution)/shard_map/psum | solution.py:72
  357.4 39.2 %psum.123 = f32[2]{0:T(128)S(1)} all-reduce(f32[2]{0:T(128)S(1)} %multiply_reduce_fusion.6), channel_id=1, replica_groups=mesh['row'=4,'col'=8] {'row','col'}, use_global_device_ids=true, to_apply=%region_9.11 | all-reduce | flops 2 | bytes 16 | tf_op jit(solution)/shard_map/psum | solution.py:76
  396.8 8.2 all_gather.26
  406.4 15.5 %convolution_bitcast_fusion.5 = f32[2,128,128]{2,0,1:T(2,128)S(1)} fusion(f32[128,128,128]{2,1,0:T(8,128)} %param.39, f32[128,2,128]{2,1,0:T(2,128)} %gather_fusion.2, pred[128]{0:T(512)(128)(4,1)S(1)} %compare_and_fusion), kind=kOutput, calls=%fused_computation.17 | convolution fusion | flops 50364416 | bytes 8650880 | tf_op jit(solution)/shard_map/kij,nkj->nki/dot_general | solution.py:44
  425.1 61.8 %reduce-scatter.13.cloned.1.call-done = f32[128,2,128]{2,0,1:T(8,128)} async-done(((f32[1024,2,128]{2,0,1:T(8,128)}), f32[128,2,128]{2,0,1:T(8,128)}) %reduce-scatter.13.cloned.1.call-update) | async-done | bytes 131088 | tf_op jit(solution)/shard_map/reduce_scatter | solution.py:45
  487.9 2.5 fusion.20
  490.4 39.8 %psum.124 = f32[2,3]{1,0:T(2,128)S(1)} all-reduce(f32[2,3]{1,0:T(2,128)S(1)} %bitcast.733), channel_id=1, replica_groups=mesh['row'=4,'col'=8] {'row','col'}, use_global_device_ids=true, to_apply=%region_12.14 | all-reduce | flops 6 | bytes 48 | tf_op jit(solution)/shard_map/psum | solution.py:72
  532.7 39.2 %psum.125 = f32[2]{0:T(128)S(1)} all-reduce(f32[2]{0:T(128)S(1)} %multiply_reduce_fusion.5), channel_id=1, replica_groups=mesh['row'=4,'col'=8] {'row','col'}, use_global_device_ids=true, to_apply=%region_14.16 | all-reduce | flops 2 | bytes 16 | tf_op jit(solution)/shard_map/psum | solution.py:76
  573.0 8.8 all_gather.27
  583.6 15.5 %convolution_bitcast_fusion.4 = f32[2,128,128]{2,0,1:T(2,128)S(1)} fusion(f32[128,128,128]{2,1,0:T(8,128)} %param.39, f32[128,2,128]{2,1,0:T(2,128)S(1)} %gather_fusion.3, pred[128]{0:T(512)(128)(4,1)S(1)} %compare_and_fusion), kind=kOutput, calls=%fused_computation.16 | convolution fusion | flops 50364416 | bytes 8650880 | tf_op jit(solution)/shard_map/kij,nkj->nki/dot_general | solution.py:44
  602.6 61.4 %reduce-scatter.15.cloned.1.call-done = f32[128,2,128]{2,0,1:T(8,128)} async-done(((f32[1024,2,128]{2,0,1:T(8,128)}), f32[128,2,128]{2,0,1:T(8,128)}) %reduce-scatter.15.cloned.1.call-update) | async-done | bytes 131088 | tf_op jit(solution)/shard_map/reduce_scatter | solution.py:45
  665.0 3.6 fusion.41
  668.6 39.8 %psum.126 = f32[2,4]{1,0:T(2,128)S(1)} all-reduce(f32[2,4]{1,0:T(2,128)S(1)} %bitcast.734), channel_id=1, replica_groups=mesh['row'=4,'col'=8] {'row','col'}, use_global_device_ids=true, to_apply=%region_17.19 | all-reduce | flops 8 | bytes 64 | tf_op jit(solution)/shard_map/psum | solution.py:72
  712.2 39.1 %psum.127 = f32[2]{0:T(128)S(1)} all-reduce(f32[2]{0:T(128)S(1)} %multiply_reduce_fusion.4), channel_id=1, replica_groups=mesh['row'=4,'col'=8] {'row','col'}, use_global_device_ids=true, to_apply=%region_19.21 | all-reduce | flops 2 | bytes 16 | tf_op jit(solution)/shard_map/psum | solution.py:76
  753.1 8.6 all_gather.28
  764.1 15.5 %convolution_bitcast_fusion.3 = f32[2,128,128]{2,0,1:T(2,128)S(1)} fusion(f32[128,128,128]{2,1,0:T(8,128)} %param.39, f32[128,2,128]{2,1,0:T(2,128)} %gather_fusion.4, pred[128]{0:T(512)(128)(4,1)S(1)} %compare_and_fusion), kind=kOutput, calls=%fused_computation.15 | convolution fusion | flops 50364416 | bytes 8650880 | tf_op jit(solution)/shard_map/kij,nkj->nki/dot_general | solution.py:44
  782.3 62.2 %reduce-scatter.17.cloned.1.call-done = f32[128,2,128]{2,0,1:T(8,128)} async-done(((f32[1024,2,128]{2,0,1:T(8,128)}), f32[128,2,128]{2,0,1:T(8,128)}) %reduce-scatter.17.cloned.1.call-update) | async-done | bytes 131088 | tf_op jit(solution)/shard_map/reduce_scatter | solution.py:45
  846.3 2.6 fusion.2
  848.9 39.8 %psum.128 = f32[2,5]{1,0:T(2,128)S(1)} all-reduce(f32[2,5]{1,0:T(2,128)S(1)} %bitcast.727), channel_id=1, replica_groups=mesh['row'=4,'col'=8] {'row','col'}, use_global_device_ids=true, to_apply=%region_22.24 | all-reduce | flops 10 | bytes 80 | tf_op jit(solution)/shard_map/psum | solution.py:72
  891.8 39.3 %psum.129 = f32[2]{0:T(128)S(1)} all-reduce(f32[2]{0:T(128)S(1)} %multiply_reduce_fusion.3), channel_id=1, replica_groups=mesh['row'=4,'col'=8] {'row','col'}, use_global_device_ids=true, to_apply=%region_24.26 | all-reduce | flops 2 | bytes 16 | tf_op jit(solution)/shard_map/psum | solution.py:76
  932.3 8.2 all_gather.29
  941.8 15.5 %convolution_bitcast_fusion.2 = f32[2,128,128]{2,0,1:T(2,128)S(1)} fusion(f32[128,128,128]{2,1,0:T(8,128)} %param.39, f32[128,2,128]{2,1,0:T(2,128)} %gather_fusion.5, pred[128]{0:T(512)(128)(4,1)S(1)} %compare_and_fusion), kind=kOutput, calls=%fused_computation.14 | convolution fusion | flops 50364416 | bytes 8650880 | tf_op jit(solution)/shard_map/kij,nkj->nki/dot_general | solution.py:44
  959.1 63.2 %reduce-scatter.19.cloned.1.call-done = f32[128,2,128]{2,0,1:T(8,128)} async-done(((f32[1024,2,128]{2,0,1:T(8,128)}), f32[128,2,128]{2,0,1:T(8,128)}) %reduce-scatter.19.cloned.1.call-update) | async-done | bytes 131088 | tf_op jit(solution)/shard_map/reduce_scatter | solution.py:45
  1023.3 2.9 fusion.6
  1026.2 39.8 %psum.130 = f32[2,6]{1,0:T(2,128)S(1)} all-reduce(f32[2,6]{1,0:T(2,128)S(1)} %bitcast.728), channel_id=1, replica_groups=mesh['row'=4,'col'=8] {'row','col'}, use_global_device_ids=true, to_apply=%region_27.29 | all-reduce | flops 12 | bytes 96 | tf_op jit(solution)/shard_map/psum | solution.py:72
  1068.3 39.2 %psum.131 = f32[2]{0:T(128)S(1)} all-reduce(f32[2]{0:T(128)S(1)} %multiply_reduce_fusion.2), channel_id=1, replica_groups=mesh['row'=4,'col'=8] {'row','col'}, use_global_device_ids=true, to_apply=%region_29.31 | all-reduce | flops 2 | bytes 16 | tf_op jit(solution)/shard_map/psum | solution.py:76
  1107.7 8.4 all_gather.30
  1116.8 15.5 %convolution_bitcast_fusion.1 = f32[2,128,128]{2,0,1:T(2,128)S(1)} fusion(f32[128,128,128]{2,1,0:T(8,128)} %param.39, f32[128,2,128]{2,1,0:T(2,128)S(1)} %gather_fusion.6, pred[128]{0:T(512)(128)(4,1)S(1)} %compare_and_fusion), kind=kOutput, calls=%fused_computation.13 | convolution fusion | flops 50364416 | bytes 8650880 | tf_op jit(solution)/shard_map/kij,nkj->nki/dot_general | solution.py:44
  1134.0 63.2 %reduce-scatter.21.cloned.1.call-done = f32[128,2,128]{2,0,1:T(8,128)} async-done(((f32[1024,2,128]{2,0,1:T(8,128)}), f32[128,2,128]{2,0,1:T(8,128)}) %reduce-scatter.21.cloned.1.call-update) | async-done | bytes 131088 | tf_op jit(solution)/shard_map/reduce_scatter | solution.py:45
  1198.3 2.9 fusion.10
  1201.2 39.9 %psum.132 = f32[2,7]{1,0:T(2,128)S(1)} all-reduce(f32[2,7]{1,0:T(2,128)S(1)} %bitcast.729), channel_id=1, replica_groups=mesh['row'=4,'col'=8] {'row','col'}, use_global_device_ids=true, to_apply=%region_32.34 | all-reduce | flops 14 | bytes 112 | tf_op jit(solution)/shard_map/psum | solution.py:72
  1242.8 39.2 %psum.133 = f32[2]{0:T(128)S(1)} all-reduce(f32[2]{0:T(128)S(1)} %multiply_reduce_fusion.1), channel_id=1, replica_groups=mesh['row'=4,'col'=8] {'row','col'}, use_global_device_ids=true, to_apply=%region_34.36 | all-reduce | flops 2 | bytes 16 | tf_op jit(solution)/shard_map/psum | solution.py:76
  1282.2 8.1 all_gather.31
  1291.1 15.5 %convolution_bitcast_fusion = f32[2,128,128]{2,0,1:T(2,128)S(1)} fusion(f32[128,128,128]{2,1,0:T(8,128)} %param.39, f32[128,2,128]{2,1,0:T(2,128)S(1)} %gather_fusion.7, pred[128]{0:T(512)(128)(4,1)S(1)} %compare_and_fusion), kind=kOutput, calls=%fused_computation.12 | convolution fusion | flops 50364416 | bytes 8650880 | tf_op jit(solution)/shard_map/kij,nkj->nki/dot_general | solution.py:44
  1332.2 39.3 %reduce-scatter.23.cloned.1.call-done = f32[128,2,128]{2,0,1:T(8,128)} async-done(((f32[1024,2,128]{2,0,1:T(8,128)}), f32[128,2,128]{2,0,1:T(8,128)}) %reduce-scatter.23.cloned.1.call-update) | async-done | bytes 131088 | tf_op jit(solution)/shard_map/reduce_scatter | solution.py:45
  1372.6 3.0 fusion.16
  1375.6 39.8 %psum.134 = f32[2,8]{1,0:T(2,128)S(1)} all-reduce(f32[2,8]{1,0:T(2,128)S(1)} %bitcast.726), channel_id=1, replica_groups=mesh['row'=4,'col'=8] {'row','col'}, use_global_device_ids=true, to_apply=%region_37.39 | all-reduce | flops 16 | bytes 128 | tf_op jit(solution)/shard_map/psum | solution.py:72
  1418.4 39.2 %psum.135 = f32[2]{0:T(128)S(1)} all-reduce(f32[2]{0:T(128)S(1)} %fusion.56), channel_id=1, replica_groups=mesh['row'=4,'col'=8] {'row','col'}, use_global_device_ids=true, to_apply=%region_39.41 | all-reduce | flops 2 | bytes 16 | tf_op jit(solution)/shard_map/psum | solution.py:76
  (181 shorter events, 97.4 us)
Async XLA Ops:
  7.2 69.7 %copy-start.8 = (s32[1,128]{1,0:T(1,128)S(1)}, s32[1,128]{1,0:T(1,128)}, u32[]{:S(2)}) copy-start(s32[1,128]{1,0:T(1,128)} %param.40) | copy-start | bytes 1540
  7.2 134.8 %copy-start = (f32[16384]{0:T(1024)S(1)}, f32[16384]{0:T(1024)}, u32[]{:S(2)}) copy-start(f32[16384]{0:T(1024)} %param.42) | copy-start | bytes 196612
  7.2 134.8 %reduce-scatter.9.cloned.1.call-start = ((), (), s32[]{:S(2)}) async-start(), calls=%async_computation.8 | async-start | bytes 1179648 | tf_op jit(solution)/shard_map/reduce_scatter | solution.py:45
  78.5 234.2 %reduce-scatter.11.cloned.1.call-start = ((), (), s32[]{:S(2)}) async-start(), calls=%async_computation.9 | async-start | bytes 1179648 | tf_op jit(solution)/shard_map/reduce_scatter | solution.py:45
  249.6 237.3 %reduce-scatter.13.cloned.1.call-start = ((), (), s32[]{:S(2)}) async-start(), calls=%async_computation.10 | async-start | bytes 1179648 | tf_op jit(solution)/shard_map/reduce_scatter | solution.py:45
  423.5 240.4 %reduce-scatter.15.cloned.1.call-start = ((), (), s32[]{:S(2)}) async-start(), calls=%async_computation.11 | async-start | bytes 1179648 | tf_op jit(solution)/shard_map/reduce_scatter | solution.py:45
  531.3 0.7 copy-start.6
  600.7 243.8 %reduce-scatter.17.cloned.1.call-start = ((), (), s32[]{:S(2)}) async-start(), calls=%async_computation.12 | async-start | bytes 1179648 | tf_op jit(solution)/shard_map/reduce_scatter | solution.py:45
  665.0 46.0 %copy-start.4 = (f32[2,16384]{1,0:T(2,128)}, f32[2,16384]{1,0:T(2,128)S(1)}, u32[]{:S(2)}) copy-start(f32[2,16384]{1,0:T(2,128)S(1)} %bitcast_add_fusion.4) | copy-start | bytes 393220
  710.8 0.6 copy-start.5
  712.2 69.1 %copy-start.1 = (f32[7,2,16384]{2,1,0:T(2,128)S(1)}, f32[7,2,16384]{2,1,0:T(2,128)}, u32[]{:S(2)}) copy-start(f32[7,2,16384]{2,1,0:T(2,128)} %get-tuple-element.273) | copy-start | bytes 2752516
  752.5 0.7 copy-start.2
  781.2 241.0 %reduce-scatter.19.cloned.1.call-start = ((), (), s32[]{:S(2)}) async-start(), calls=%async_computation.13 | async-start | bytes 1179648 | tf_op jit(solution)/shard_map/reduce_scatter | solution.py:45
  845.6 0.7 copy-start.3
  890.0 0.6 copy-start.7
  958.9 238.3 %reduce-scatter.21.cloned.1.call-start = ((), (), s32[]{:S(2)}) async-start(), calls=%async_computation.14 | async-start | bytes 1179648 | tf_op jit(solution)/shard_map/reduce_scatter | solution.py:45
  1133.8 175.5 %copy-start.14 = (s32[3]{0:T(128)S(1)}, s32[3]{0:T(128)}, u32[]{:S(2)}) copy-start(s32[3]{0:T(128)} %constant.460.clone.1) | copy-start | bytes 40
  1133.9 176.2 %copy-start.13 = (s32[3]{0:T(128)S(1)}, s32[3]{0:T(128)}, u32[]{:S(2)}) copy-start(s32[3]{0:T(128)} %constant.463.clone.1) | copy-start | bytes 40
  1133.9 177.0 %copy-start.12 = (s32[3]{0:T(128)S(1)}, s32[3]{0:T(128)}, u32[]{:S(2)}) copy-start(s32[3]{0:T(128)} %constant.465.clone.1) | copy-start | bytes 40
  1133.9 177.7 %copy-start.11 = (s32[3]{0:T(128)S(1)}, s32[3]{0:T(128)}, u32[]{:S(2)}) copy-start(s32[3]{0:T(128)} %constant.467.clone.1) | copy-start | bytes 40
  1133.9 178.5 %copy-start.10 = (s32[3]{0:T(128)S(1)}, s32[3]{0:T(128)}, u32[]{:S(2)}) copy-start(s32[3]{0:T(128)} %constant.469.clone.1) | copy-start | bytes 40
  1133.9 179.2 %copy-start.9 = (s32[3]{0:T(128)S(1)}, s32[3]{0:T(128)}, u32[]{:S(2)}) copy-start(s32[3]{0:T(128)} %constant.471.clone.1) | copy-start | bytes 40
  1133.9 237.6 %reduce-scatter.23.cloned.1.call-start = ((), (), s32[]{:S(2)}) async-start(), calls=%async_computation.15 | async-start | bytes 1179648 | tf_op jit(solution)/shard_map/reduce_scatter | solution.py:45
Sparse Core Ops, SparseCore 0:
  78.6 63.3 reduce-scatter.8
  249.7 62.9 reduce-scatter.10
  423.6 63.1 reduce-scatter.12
  600.8 63.0 reduce-scatter.14
  781.3 63.1 reduce-scatter.16
  959.1 63.1 reduce-scatter.18
  1134.0 63.1 reduce-scatter.20
  1308.3 63.1 reduce-scatter.22
where the time goes:
time: 1480 us; the launch traced here: 1470 us
  blocking collectives  740 us (50%)
  waiting for transfers between devices  476 us (32%)
  matrix products  168 us (11%)
  other arithmetic  38.8 us (3%)
  local copies, waits for them, and re-layouts  33.9 us (2%)
  between operations  14.8 us (1%)
    reduce_scatter x8, waiting for transfers between devices, apply_matrix(): lax.psum_scatter(jnp.einsum('mk,nki->mni', rows_onehot, products, precisi...  475 us
    psum x8, blocking collectives, body(): coeffs = lax.psum(local_dots, ('row', 'col'))  319 us
    psum x8, blocking collectives, body(): lax.psum(jnp.sum(candidate * candidate, axis=1), ('row', 'col'))  314 us
    dot_general x8, matrix products, apply_matrix(): jnp.einsum('kij,nkj->nki', blocks, picked, precision=lax.Precision.HIGHEST)  124 us
    all_gather x8, blocking collectives, apply_matrix(): gathered = lax.all_gather(vector, 'row', axis=1, tiled=True)  66.2 us
    psum x1, blocking collectives, body(): lax.psum(jnp.sum(right_sides * right_sides, axis=1), ('row', 'col'))  41.9 us
  transfers between devices with their start and end apart: 8, of which 8 were waited for; matrix products, arithmetic and copies ran while one was open for 2% of the time, Pallas kernels for 0%

commit v1 on v0

--- a/solution.py
+++ b/solution.py
@@ -73,7 +73,8 @@
         candidate = candidate - jnp.einsum(
             "ni,inl->nl", coeffs, stacked, precision=lax.Precision.HIGHEST
         )
-        remainder_sq = lax.psum(jnp.sum(candidate * candidate, axis=1), ("row", "col"))
+        half = lax.psum(jnp.sum(candidate * candidate, axis=1), "row")
+        remainder_sq = lax.psum(half, "col")
         new_norm = jnp.sqrt(remainder_sq + epsilon)
         hessenberg = hessenberg.at[:, : j + 1, j].set(coeffs)
         hessenberg = hessenberg.at[:, j + 1, j].set(new_norm)

time: 1480 us -> 1350 us (0.912)
  blocking collectives: 740 us -> 626 us
    psum x8 -> x16, blocking collectives: 314 us -> 210 us  [the longest x8 164 us: body(): remainder_sq = lax.psum(half, 'col')]
where the time goes in v1:
time: 1350 us; the launch traced here: 1340 us
  blocking collectives  626 us (46%)
  waiting for transfers between devices  466 us (35%)
  matrix products  169 us (13%)
  other arithmetic  36.5 us (3%)
  local copies, waits for them, and re-layouts  28 us (2%)
  between operations  14.7 us (1%)
    reduce_scatter x8, waiting for transfers between devices, apply_matrix(): lax.psum_scatter(jnp.einsum('mk,nki->mni', rows_onehot, products, precisi...  466 us
    psum x8, blocking collectives, body(): coeffs = lax.psum(local_dots, ('row', 'col'))  319 us
    psum x8, blocking collectives, body(): remainder_sq = lax.psum(half, 'col')  164 us
    dot_general x8, matrix products, apply_matrix(): jnp.einsum('kij,nkj->nki', blocks, picked, precision=lax.Precision.HIGHEST)  124 us
    all_gather x8, blocking collectives, apply_matrix(): gathered = lax.all_gather(vector, 'row', axis=1, tiled=True)  55.7 us
    psum x8, blocking collectives, body(): half = lax.psum(jnp.sum(candidate * candidate, axis=1), 'row')  46.4 us
    psum x1, blocking collectives, body(): lax.psum(jnp.sum(right_sides * right_sides, axis=1), ('row', 'col'))  41.9 us
  transfers between devices with their start and end apart: 8, of which 8 were waited for; matrix products, arithmetic and copies ran while one was open for 2% of the time, Pallas kernels for 0%

profile of v1, /device:TPU:0, one launch (start us, length us, event | category | flops | bytes accessed | tf_op | source)
XLA Modules:
  0.0 1340.4 jit_solution(7146938113595902983)
XLA Ops:
  9.7 41.9 %psum.175 = f32[2]{0:T(128)S(1)} all-reduce(f32[2]{0:T(128)S(1)} %multiply_reduce_fusion.8), channel_id=1, replica_groups=mesh['row'=4,'col'=8] {'row','col'}, use_global_device_ids=true, to_apply=%region_1.0 | all-reduce | flops 2 | bytes 16 | tf_op jit(solution)/shard_map/psum | solution.py:64
  52.7 7.9 all_gather.24
  61.4 15.5 %convolution_bitcast_fusion.7 = f32[2,128,128]{2,0,1:T(2,128)S(1)} fusion(f32[128,128,128]{2,1,0:T(8,128)} %param.39, f32[128,2,128]{2,1,0:T(2,128)S(1)} %gather_fusion, pred[128]{0:T(512)(128)(4,1)S(1)} %compare_and_fusion), kind=kOutput, calls=%fused_computation.19 | convolution fusion | flops 50364416 | bytes 8650880 | tf_op jit(solution)/shard_map/kij,nkj->nki/dot_general | solution.py:44
  78.5 63.3 %reduce-scatter.9.cloned.1.call-done = f32[128,2,128]{2,0,1:T(8,128)} async-done(((f32[1024,2,128]{2,0,1:T(8,128)}), f32[128,2,128]{2,0,1:T(8,128)}) %reduce-scatter.9.cloned.1.call-update) | async-done | bytes 131088 | tf_op jit(solution)/shard_map/reduce_scatter | solution.py:45
  142.9 39.9 %psum.176 = f32[2,1]{0,1:T(1,128)S(1)} all-reduce(f32[2,1]{0,1:T(1,128)S(1)} %bitcast.742), channel_id=1, replica_groups=mesh['row'=4,'col'=8] {'row','col'}, use_global_device_ids=true, to_apply=%region_3.5 | all-reduce | flops 2 | bytes 16 | tf_op jit(solution)/shard_map/psum | solution.py:72
  184.0 5.8 psum.177
  189.8 20.6 %psum.178 = f32[2]{0:T(128)S(1)} all-reduce(f32[2]{0:T(128)S(1)} %psum.177), channel_id=1, replica_groups=mesh['row'=4,'col'=8] {'col'}, use_global_device_ids=true, to_apply=%region_6.8 | all-reduce | flops 2 | bytes 16 | tf_op jit(solution)/shard_map/psum | solution.py:77
  210.6 6.7 all_gather.25
  218.0 15.5 %convolution_bitcast_fusion.6 = f32[2,128,128]{2,0,1:T(2,128)S(1)} fusion(f32[128,128,128]{2,1,0:T(8,128)} %param.39, f32[128,2,128]{2,1,0:T(2,128)S(1)} %gather_fusion.1, pred[128]{0:T(512)(128)(4,1)S(1)} %compare_and_fusion), kind=kOutput, calls=%fused_computation.18 | convolution fusion | flops 50364416 | bytes 8650880 | tf_op jit(solution)/shard_map/kij,nkj->nki/dot_general | solution.py:44
  235.3 61.1 %reduce-scatter.11.cloned.1.call-done = f32[128,2,128]{2,0,1:T(8,128)} async-done(((f32[1024,2,128]{2,0,1:T(8,128)}), f32[128,2,128]{2,0,1:T(8,128)}) %reduce-scatter.11.cloned.1.call-update) | async-done | bytes 131088 | tf_op jit(solution)/shard_map/reduce_scatter | solution.py:45
  299.9 39.8 %psum.179 = f32[2,2]{1,0:T(2,128)S(1)} all-reduce(f32[2,2]{1,0:T(2,128)S(1)} %bitcast.732), channel_id=1, replica_groups=mesh['row'=4,'col'=8] {'row','col'}, use_global_device_ids=true, to_apply=%region_8.10 | all-reduce | flops 4 | bytes 32 | tf_op jit(solution)/shard_map/psum | solution.py:72
  341.1 5.8 psum.180
  346.9 20.2 %psum.181 = f32[2]{0:T(128)S(1)} all-reduce(f32[2]{0:T(128)S(1)} %psum.180), channel_id=1, replica_groups=mesh['row'=4,'col'=8] {'col'}, use_global_device_ids=true, to_apply=%region_11.13 | all-reduce | flops 2 | bytes 16 | tf_op jit(solution)/shard_map/psum | solution.py:77
  367.3 6.7 all_gather.26
  374.8 15.5 %convolution_bitcast_fusion.5 = f32[2,128,128]{2,0,1:T(2,128)S(1)} fusion(f32[128,128,128]{2,1,0:T(8,128)} %param.39, f32[128,2,128]{2,1,0:T(2,128)S(1)} %gather_fusion.2, pred[128]{0:T(512)(128)(4,1)S(1)} %compare_and_fusion), kind=kOutput, calls=%fused_computation.17 | convolution fusion | flops 50364416 | bytes 8650880 | tf_op jit(solution)/shard_map/kij,nkj->nki/dot_general | solution.py:44
  393.4 59.7 %reduce-scatter.13.cloned.1.call-done = f32[128,2,128]{2,0,1:T(8,128)} async-done(((f32[1024,2,128]{2,0,1:T(8,128)}), f32[128,2,128]{2,0,1:T(8,128)}) %reduce-scatter.13.cloned.1.call-update) | async-done | bytes 131088 | tf_op jit(solution)/shard_map/reduce_scatter | solution.py:45
  456.7 39.8 %psum.182 = f32[2,3]{1,0:T(2,128)S(1)} all-reduce(f32[2,3]{1,0:T(2,128)S(1)} %bitcast.733), channel_id=1, replica_groups=mesh['row'=4,'col'=8] {'row','col'}, use_global_device_ids=true, to_apply=%region_14.16 | all-reduce | flops 6 | bytes 48 | tf_op jit(solution)/shard_map/psum | solution.py:72
  500.1 5.8 psum.183
  505.9 20.6 %psum.184 = f32[2]{0:T(128)S(1)} all-reduce(f32[2]{0:T(128)S(1)} %psum.183), channel_id=1, replica_groups=mesh['row'=4,'col'=8] {'col'}, use_global_device_ids=true, to_apply=%region_17.19 | all-reduce | flops 2 | bytes 16 | tf_op jit(solution)/shard_map/psum | solution.py:77
  527.6 7.4 all_gather.27
  536.7 15.5 %convolution_bitcast_fusion.4 = f32[2,128,128]{2,0,1:T(2,128)S(1)} fusion(f32[128,128,128]{2,1,0:T(8,128)} %param.39, f32[128,2,128]{2,1,0:T(2,128)S(1)} %gather_fusion.3, pred[128]{0:T(512)(128)(4,1)S(1)} %compare_and_fusion), kind=kOutput, calls=%fused_computation.16 | convolution fusion | flops 50364416 | bytes 8650880 | tf_op jit(solution)/shard_map/kij,nkj->nki/dot_general | solution.py:44
  555.7 59.5 %reduce-scatter.15.cloned.1.call-done = f32[128,2,128]{2,0,1:T(8,128)} async-done(((f32[1024,2,128]{2,0,1:T(8,128)}), f32[128,2,128]{2,0,1:T(8,128)}) %reduce-scatter.15.cloned.1.call-update) | async-done | bytes 131088 | tf_op jit(solution)/shard_map/reduce_scatter | solution.py:45
  619.8 39.8 %psum.185 = f32[2,4]{1,0:T(2,128)S(1)} all-reduce(f32[2,4]{1,0:T(2,128)S(1)} %bitcast.734), channel_id=1, replica_groups=mesh['row'=4,'col'=8] {'row','col'}, use_global_device_ids=true, to_apply=%region_20.22 | all-reduce | flops 8 | bytes 64 | tf_op jit(solution)/shard_map/psum | solution.py:72
  669.5 20.5 %psum.187 = f32[2]{0:T(128)S(1)} all-reduce(f32[2]{0:T(128)S(1)} %psum.186), channel_id=1, replica_groups=mesh['row'=4,'col'=8] {'col'}, use_global_device_ids=true, to_apply=%region_23.25 | all-reduce | flops 2 | bytes 16 | tf_op jit(solution)/shard_map/psum | solution.py:77
  690.2 6.7 all_gather.28
  697.6 15.5 %convolution_bitcast_fusion.3 = f32[2,128,128]{2,0,1:T(2,128)S(1)} fusion(f32[128,128,128]{2,1,0:T(8,128)} %param.39, f32[128,2,128]{2,1,0:T(2,128)S(1)} %gather_fusion.4, pred[128]{0:T(512)(128)(4,1)S(1)} %compare_and_fusion), kind=kOutput, calls=%fused_computation.15 | convolution fusion | flops 50364416 | bytes 8650880 | tf_op jit(solution)/shard_map/kij,nkj->nki/dot_general | solution.py:44
  715.5 60.5 %reduce-scatter.17.cloned.1.call-done = f32[128,2,128]{2,0,1:T(8,128)} async-done(((f32[1024,2,128]{2,0,1:T(8,128)}), f32[128,2,128]{2,0,1:T(8,128)}) %reduce-scatter.17.cloned.1.call-update) | async-done | bytes 131088 | tf_op jit(solution)/shard_map/reduce_scatter | solution.py:45
  779.7 39.8 %psum.188 = f32[2,5]{1,0:T(2,128)S(1)} all-reduce(f32[2,5]{1,0:T(2,128)S(1)} %bitcast.727), channel_id=1, replica_groups=mesh['row'=4,'col'=8] {'row','col'}, use_global_device_ids=true, to_apply=%region_26.28 | all-reduce | flops 10 | bytes 80 | tf_op jit(solution)/shard_map/psum | solution.py:72
  821.7 5.8 psum.189
  827.5 20.6 %psum.190 = f32[2]{0:T(128)S(1)} all-reduce(f32[2]{0:T(128)S(1)} %psum.189), channel_id=1, replica_groups=mesh['row'=4,'col'=8] {'col'}, use_global_device_ids=true, to_apply=%region_29.31 | all-reduce | flops 2 | bytes 16 | tf_op jit(solution)/shard_map/psum | solution.py:77
  848.3 6.7 all_gather.29
  856.4 15.5 %convolution_bitcast_fusion.2 = f32[2,128,128]{2,0,1:T(2,128)S(1)} fusion(f32[128,128,128]{2,1,0:T(8,128)} %param.39, f32[128,2,128]{2,1,0:T(2,128)} %gather_fusion.5, pred[128]{0:T(512)(128)(4,1)S(1)} %compare_and_fusion), kind=kOutput, calls=%fused_computation.14 | convolution fusion | flops 50364416 | bytes 8650880 | tf_op jit(solution)/shard_map/kij,nkj->nki/dot_general | solution.py:44
  873.7 61.2 %reduce-scatter.19.cloned.1.call-done = f32[128,2,128]{2,0,1:T(8,128)} async-done(((f32[1024,2,128]{2,0,1:T(8,128)}), f32[128,2,128]{2,0,1:T(8,128)}) %reduce-scatter.19.cloned.1.call-update) | async-done | bytes 131088 | tf_op jit(solution)/shard_map/reduce_scatter | solution.py:45
  938.8 39.8 %psum.191 = f32[2,6]{1,0:T(2,128)S(1)} all-reduce(f32[2,6]{1,0:T(2,128)S(1)} %bitcast.728), channel_id=1, replica_groups=mesh['row'=4,'col'=8] {'row','col'}, use_global_device_ids=true, to_apply=%region_32.34 | all-reduce | flops 12 | bytes 96 | tf_op jit(solution)/shard_map/psum | solution.py:72
  980.9 5.8 psum.192
  986.7 20.5 %psum.193 = f32[2]{0:T(128)S(1)} all-reduce(f32[2]{0:T(128)S(1)} %psum.192), channel_id=1, replica_groups=mesh['row'=4,'col'=8] {'col'}, use_global_device_ids=true, to_apply=%region_35.37 | all-reduce | flops 2 | bytes 16 | tf_op jit(solution)/shard_map/psum | solution.py:77
  1007.4 7.0 all_gather.30
  1015.1 15.5 %convolution_bitcast_fusion.1 = f32[2,128,128]{2,0,1:T(2,128)S(1)} fusion(f32[128,128,128]{2,1,0:T(8,128)} %param.39, f32[128,2,128]{2,1,0:T(2,128)S(1)} %gather_fusion.6, pred[128]{0:T(512)(128)(4,1)S(1)} %compare_and_fusion), kind=kOutput, calls=%fused_computation.13 | convolution fusion | flops 50364416 | bytes 8650880 | tf_op jit(solution)/shard_map/kij,nkj->nki/dot_general | solution.py:44
  1032.3 61.2 %reduce-scatter.21.cloned.1.call-done = f32[128,2,128]{2,0,1:T(8,128)} async-done(((f32[1024,2,128]{2,0,1:T(8,128)}), f32[128,2,128]{2,0,1:T(8,128)}) %reduce-scatter.21.cloned.1.call-update) | async-done | bytes 131088 | tf_op jit(solution)/shard_map/reduce_scatter | solution.py:45
  1097.5 39.8 %psum.194 = f32[2,7]{1,0:T(2,128)S(1)} all-reduce(f32[2,7]{1,0:T(2,128)S(1)} %bitcast.729), channel_id=1, replica_groups=mesh['row'=4,'col'=8] {'row','col'}, use_global_device_ids=true, to_apply=%region_38.40 | all-reduce | flops 14 | bytes 112 | tf_op jit(solution)/shard_map/psum | solution.py:72
  1139.7 5.8 psum.195
  1145.5 20.2 %psum.196 = f32[2]{0:T(128)S(1)} all-reduce(f32[2]{0:T(128)S(1)} %psum.195), channel_id=1, replica_groups=mesh['row'=4,'col'=8] {'col'}, use_global_device_ids=true, to_apply=%region_41.43 | all-reduce | flops 2 | bytes 16 | tf_op jit(solution)/shard_map/psum | solution.py:77
  1165.9 6.7 all_gather.31
  1173.4 15.5 %convolution_bitcast_fusion = f32[2,128,128]{2,0,1:T(2,128)S(1)} fusion(f32[128,128,128]{2,1,0:T(8,128)} %param.39, f32[128,2,128]{2,1,0:T(2,128)S(1)} %gather_fusion.7, pred[128]{0:T(512)(128)(4,1)S(1)} %compare_and_fusion), kind=kOutput, calls=%fused_computation.12 | convolution fusion | flops 50364416 | bytes 8650880 | tf_op jit(solution)/shard_map/kij,nkj->nki/dot_general | solution.py:44
  1212.6 39.1 %reduce-scatter.23.cloned.1.call-done = f32[128,2,128]{2,0,1:T(8,128)} async-done(((f32[1024,2,128]{2,0,1:T(8,128)}), f32[128,2,128]{2,0,1:T(8,128)}) %reduce-scatter.23.cloned.1.call-update) | async-done | bytes 131088 | tf_op jit(solution)/shard_map/reduce_scatter | solution.py:45
  1255.8 39.8 %psum.197 = f32[2,8]{1,0:T(2,128)S(1)} all-reduce(f32[2,8]{1,0:T(2,128)S(1)} %bitcast.726), channel_id=1, replica_groups=mesh['row'=4,'col'=8] {'row','col'}, use_global_device_ids=true, to_apply=%region_44.46 | all-reduce | flops 16 | bytes 128 | tf_op jit(solution)/shard_map/psum | solution.py:72
  1299.6 5.8 psum.198
  1305.4 20.6 %psum.199 = f32[2]{0:T(128)S(1)} all-reduce(f32[2]{0:T(128)S(1)} %psum.198), channel_id=1, replica_groups=mesh['row'=4,'col'=8] {'col'}, use_global_device_ids=true, to_apply=%region_47.49 | all-reduce | flops 2 | bytes 16 | tf_op jit(solution)/shard_map/psum | solution.py:77
  (177 shorter events, 115.7 us)
Async XLA Ops:
  7.2 69.7 %copy-start.2 = (s32[1,128]{1,0:T(1,128)S(1)}, s32[1,128]{1,0:T(1,128)}, u32[]{:S(2)}) copy-start(s32[1,128]{1,0:T(1,128)} %param.40) | copy-start | bytes 1540
  7.2 134.6 %copy-start = (f32[16384]{0:T(1024)S(1)}, f32[16384]{0:T(1024)}, u32[]{:S(2)}) copy-start(f32[16384]{0:T(1024)} %param.42) | copy-start | bytes 196612
  7.2 134.6 %reduce-scatter.9.cloned.1.call-start = ((), (), s32[]{:S(2)}) async-start(), calls=%async_computation.8 | async-start | bytes 1179648 | tf_op jit(solution)/shard_map/reduce_scatter | solution.py:45
  78.5 217.9 %reduce-scatter.11.cloned.1.call-start = ((), (), s32[]{:S(2)}) async-start(), calls=%async_computation.9 | async-start | bytes 1179648 | tf_op jit(solution)/shard_map/reduce_scatter | solution.py:45
  235.1 218.1 %reduce-scatter.13.cloned.1.call-start = ((), (), s32[]{:S(2)}) async-start(), calls=%async_computation.10 | async-start | bytes 1179648 | tf_op jit(solution)/shard_map/reduce_scatter | solution.py:45
  391.8 223.3 %reduce-scatter.15.cloned.1.call-start = ((), (), s32[]{:S(2)}) async-start(), calls=%async_computation.11 | async-start | bytes 1179648 | tf_op jit(solution)/shard_map/reduce_scatter | solution.py:45
  553.8 222.2 %reduce-scatter.17.cloned.1.call-start = ((), (), s32[]{:S(2)}) async-start(), calls=%async_computation.12 | async-start | bytes 1179648 | tf_op jit(solution)/shard_map/reduce_scatter | solution.py:45
  714.7 220.1 %reduce-scatter.19.cloned.1.call-start = ((), (), s32[]{:S(2)}) async-start(), calls=%async_computation.13 | async-start | bytes 1179648 | tf_op jit(solution)/shard_map/reduce_scatter | solution.py:45
  820.9 52.7 %copy-start.1 = (f32[7,2,16384]{2,1,0:T(2,128)S(1)}, f32[7,2,16384]{2,1,0:T(2,128)}, u32[]{:S(2)}) copy-start(f32[7,2,16384]{2,1,0:T(2,128)} %get-tuple-element.270) | copy-start | bytes 2752516
  873.5 220.0 %reduce-scatter.21.cloned.1.call-start = ((), (), s32[]{:S(2)}) async-start(), calls=%async_computation.14 | async-start | bytes 1179648 | tf_op jit(solution)/shard_map/reduce_scatter | solution.py:45
  1032.2 159.5 %copy-start.8 = (s32[3]{0:T(128)S(1)}, s32[3]{0:T(128)}, u32[]{:S(2)}) copy-start(s32[3]{0:T(128)} %constant.460.clone.1) | copy-start | bytes 40
  1032.2 160.2 %copy-start.7 = (s32[3]{0:T(128)S(1)}, s32[3]{0:T(128)}, u32[]{:S(2)}) copy-start(s32[3]{0:T(128)} %constant.463.clone.1) | copy-start | bytes 40
  1032.2 160.9 %copy-start.6 = (s32[3]{0:T(128)S(1)}, s32[3]{0:T(128)}, u32[]{:S(2)}) copy-start(s32[3]{0:T(128)} %constant.465.clone.1) | copy-start | bytes 40
  1032.2 161.6 %copy-start.5 = (s32[3]{0:T(128)S(1)}, s32[3]{0:T(128)}, u32[]{:S(2)}) copy-start(s32[3]{0:T(128)} %constant.467.clone.1) | copy-start | bytes 40
  1032.2 162.4 %copy-start.4 = (s32[3]{0:T(128)S(1)}, s32[3]{0:T(128)}, u32[]{:S(2)}) copy-start(s32[3]{0:T(128)} %constant.469.clone.1) | copy-start | bytes 40
  1032.2 163.1 %copy-start.3 = (s32[3]{0:T(128)S(1)}, s32[3]{0:T(128)}, u32[]{:S(2)}) copy-start(s32[3]{0:T(128)} %constant.471.clone.1) | copy-start | bytes 40
  1032.2 219.4 %reduce-scatter.23.cloned.1.call-start = ((), (), s32[]{:S(2)}) async-start(), calls=%async_computation.15 | async-start | bytes 1179648 | tf_op jit(solution)/shard_map/reduce_scatter | solution.py:45
Sparse Core Ops, SparseCore 0:
  78.6 63.1 reduce-scatter.8
  235.2 61.1 reduce-scatter.10
  392.0 61.1 reduce-scatter.12
  553.9 61.2 reduce-scatter.14
  714.8 61.1 reduce-scatter.16
  873.6 61.1 reduce-scatter.18
  1032.4 61.1 reduce-scatter.20
  1190.6 61.0 reduce-scatter.22
